TPU v7x, 256 devices: a 4x2x16 block of a 4x16x16 slice. The times are simulated.
256 devices in a mesh: rep: 2 (over y), ep: 16 (over z), tp: 8 (over x, core).
Axes of the slice: x: 4, y: 2, z: 16, core: 2. Of those that a mesh axis runs over, the one named last changes fastest.
The devices are a block of a 4x16x16 slice.
Arguments:
- residual_in: bfloat16 [4096, 4096], P(('rep', 'ep'), 'tp'), parts along dimension 0, may hold values from -3.2 to 3.2
- queries: bfloat16 [4096, 4096], P(('rep', 'ep'), 'tp'), parts along dimension 0, may hold values from -120 to 120
- key_rows: bfloat16 [4096, 256], P(('rep', 'ep')), parts along dimension 0, may hold values from -4 to 4
- value_rows: bfloat16 [4096, 256], P(('rep', 'ep')), parts along dimension 0, may hold values from -6 to 6
- seq_lengths: int32 [32], P(('rep', 'ep')), parts along dimension 0, may hold values from 64 to 128
- out_weight: bfloat16 [4096, 4096], P('tp', 'ep'), may hold values from -0.09375 to 0.09375
- norm_gain: float32 [4096], P('tp'), may hold values from 0.25 to 1.75
- expert_ids: int32 [4096, 8], P(('rep', 'ep')), parts along dimension 0, may hold values from 0 to 31, all different within a row; in each aligned block of 128 rows (0 to 127, 128 to 255, ...) at most 48 rows name the same one
- gate_probs: float32 [4096, 8], P(('rep', 'ep')), parts along dimension 0, may hold values from 0.03 to 0.5
- gate_weight: bfloat16 [32, 4096, 1536], P('ep', None, 'tp'), may hold values from -0.09375 to 0.09375
- up_weight: bfloat16 [32, 4096, 1536], P('ep', None, 'tp'), may hold values from -0.09375 to 0.09375
- down_weight: bfloat16 [32, 1536, 4096], P('ep', None, 'tp'), may hold values from -0.15625 to 0.15625
Outputs:
- layer_out: bfloat16 [4096, 4096], P(('rep', 'ep'), 'tp'), parts along dimension 0
There are 2 independent parts, one for each index of `rep`. A program takes and returns all parts, laid end to end along the dimension named above; an argument that names none is the same for every part. Nothing has to cross between parts.
Inputs may be any that keep to these rules, and one draw needn't show every extreme that they name: `expert_ids`: each row names 8 different experts. Within the rows of one sequence no expert is named by more than 48 rows, a bound that some block reaches. `seq_lengths`: each sequence's number of valid tokens.
All inputs are finite; a program needn't handle non-finite values.
Results may differ from a plain program's by a relative error of at most 0.015.
Values may be sent and summed in bfloat16 or wider, within the bound.
No kernel may reach another device: no remote copies, remote signals or barrier semaphores. Data moves between devices by JAX's collectives and lax.ppermute only.
A program may use at most 128 MiB of HBM per device.

v0:
```python
import jax
import jax.numpy as jnp
from jax import lax
from jax.sharding import PartitionSpec as P

D = 4096
HEADS = 32
KV_HEADS = 2
HEAD_DIM = 128
EPSILON = 1e-06


def in_blocks(x, dim, count):
    before, after = (x.shape[:dim], x.shape[dim + 1 :])
    return jnp.moveaxis(x.reshape(*before, count, -1, *after), dim, 0)


def sent_and_summed(x, axis, dim):
    blocks = in_blocks(x, dim, lax.axis_size(axis))
    arrived = lax.all_to_all(blocks, axis, split_axis=0, concat_axis=0, tiled=True)
    return arrived.astype(jnp.float32).sum(axis=0)


def sent_to_all(x, axis):
    count = lax.axis_size(axis)
    return lax.all_to_all(jnp.broadcast_to(x[None], (count, *x.shape)), axis, 0, 0, tiled=True)


def over_copies(x, axis):
    everything = sent_to_all(x, axis)
    return jnp.sum(everything, axis=0)


def attend(queries, key_rows, value_rows, seq_lengths):
    seq_rows = queries.shape[0]
    heads_here = queries.shape[1] // HEAD_DIM
    group_size = HEADS // KV_HEADS
    kv_column = lax.axis_index("tp") * heads_here // group_size * HEAD_DIM
    key_head = lax.dynamic_slice_in_dim(key_rows, kv_column, HEAD_DIM, 1)
    value_head = lax.dynamic_slice_in_dim(value_rows, kv_column, HEAD_DIM, 1)
    query_three = queries.reshape(seq_rows, heads_here, HEAD_DIM)
    scores = jnp.einsum(
        "qhd,kd->hqk", query_three, key_head, preferred_element_type=jnp.float32
    ) * HEAD_DIM ** (-0.5)
    positions = jnp.arange(seq_rows, dtype=jnp.int32)
    visible = (positions[None, :] <= positions[:, None]) & (positions[None, :] < seq_lengths[0])
    scores = jnp.where(visible[None, :, :], scores, jnp.float32(-1e30))
    row_peak = jnp.max(scores, axis=2, keepdims=True)
    exponent = jnp.exp(scores - row_peak)
    weights = (exponent / jnp.sum(exponent, axis=2, keepdims=True)).astype(jnp.bfloat16)
    combined = jnp.einsum("hqk,kd->qhd", weights, value_head, preferred_element_type=jnp.float32)
    return combined.astype(jnp.bfloat16).reshape(seq_rows, heads_here * HEAD_DIM)


def shards(
    residual_in,
    queries,
    key_rows,
    value_rows,
    seq_lengths,
    out_weight,
    norm_gain,
    expert_ids,
    gate_probs,
    gate_weight,
    up_weight,
    down_weight,
):
    seq_rows = residual_in.shape[0]
    attended = attend(queries, key_rows, value_rows, seq_lengths)
    projected = jnp.dot(
        attended,
        lax.all_gather(out_weight, "ep", axis=1, tiled=True),
        preferred_element_type=jnp.float32,
    )
    head_total = sent_and_summed(projected.astype(jnp.bfloat16), "tp", 1)
    residual = (residual_in.astype(jnp.float32) + head_total).astype(jnp.bfloat16)
    residual_wide = residual.astype(jnp.float32)
    square_sum = over_copies(jnp.sum(residual_wide * residual_wide, axis=1), "tp")
    mean_square = square_sum / D
    normed = (residual_wide * lax.rsqrt(mean_square + EPSILON)[:, None] * norm_gain).astype(
        jnp.bfloat16
    )
    top_count = expert_ids.shape[1]
    local_experts = gate_weight.shape[0]
    ep_count = lax.axis_size("ep")
    expert_count = local_experts * ep_count
    capacity = min(seq_rows, 3 * seq_rows * top_count // (2 * expert_count))
    flat_ids = expert_ids.reshape(-1)
    one_hot = (flat_ids[:, None] == jnp.arange(expert_count, dtype=jnp.int32)[None, :]).astype(
        jnp.int32
    )
    earlier = jnp.cumsum(one_hot, axis=0) - one_hot
    slot_rank = jnp.sum(earlier * one_hot, axis=1)
    target = flat_ids * capacity + slot_rank
    pair_token = jnp.arange(seq_rows * top_count, dtype=jnp.int32) // top_count
    token_of = jnp.zeros((expert_count * capacity,), jnp.int32).at[target].set(pair_token)
    filled = jnp.zeros((expert_count * capacity,), jnp.bool_).at[target].set(True)
    taken = jnp.where(
        filled[:, None], jnp.take(normed, token_of, axis=0), jnp.zeros((), normed.dtype)
    )
    arrived = lax.all_gather(
        lax.all_to_all(
            taken.reshape(ep_count, local_experts, capacity, normed.shape[1]),
            "ep",
            split_axis=0,
            concat_axis=0,
            tiled=True,
        ),
        "tp",
        axis=3,
        tiled=True,
    )
    gate_val = jnp.einsum(
        "secd,edf->secf", arrived, gate_weight, preferred_element_type=jnp.float32
    )
    up_val = jnp.einsum("secd,edf->secf", arrived, up_weight, preferred_element_type=jnp.float32)
    active = (jax.nn.silu(gate_val) * up_val).astype(jnp.bfloat16)
    hidden_all = lax.all_gather(active, "tp", axis=3, tiled=True)
    produced = jnp.einsum(
        "secf,efd->secd", hidden_all, down_weight, preferred_element_type=jnp.float32
    )
    returned_rows = lax.all_to_all(
        produced.astype(jnp.bfloat16), "ep", split_axis=0, concat_axis=0, tiled=True
    ).astype(produced.dtype)
    flat_back = returned_rows.reshape(expert_count * capacity, returned_rows.shape[3])
    picked = jnp.take(flat_back, target, axis=0).reshape(seq_rows, top_count, flat_back.shape[1])
    mixture = jnp.einsum("tk,tkd->td", gate_probs, picked)
    return (residual_wide + mixture).astype(jnp.bfloat16)


def solution(mesh):
    return jax.shard_map(
        shards,
        mesh=mesh,
        in_specs=(
            P(("rep", "ep"), "tp"),
            P(("rep", "ep"), "tp"),
            P(("rep", "ep"), None),
            P(("rep", "ep"), None),
            P(("rep", "ep")),
            P("tp", "ep"),
            P("tp"),
            P(("rep", "ep"), None),
            P(("rep", "ep"), None),
            P("ep", None, "tp"),
            P("ep", None, "tp"),
            P("ep", None, "tp"),
        ),
        out_specs=P(("rep", "ep"), "tp"),
        check_vma=False,
    )
```

profile of v0, /device:TPU:40, one launch (start us, length us, event | category | flops | bytes accessed | tf_op | source)
XLA Modules:
  0.0 519.2 jit_solution(854462992069098859)
XLA Ops:
  6.6 0.7 all-gather.4.cloned.1.call-update
  8.1 0.8 copy.73
  8.9 0.1 eq.26
  9.0 9.0 %reduce-window.6 = s32[32,8,128]{2,1,0:T(8,128)S(1)} reduce-window(s32[32,8,128]{2,1,0:T(8,128)S(1)} %fusion.40, s32[]{:T(128)} %constant.48.clone.1), window={size=1x1x128 pad=0_0x0_0x127_0}, to_apply=%region_3.4 | reduce-window | flops 4161536 | bytes 262148 | tf_op jit(solution)/shard_map/reduce-window
  18.0 0.1 slice.12
  18.1 0.1 copy.75
  18.4 0.1 fusion.41
  18.5 1.2 fusion.65
  19.7 1.8 fusion.27
  21.5 1.9 convolution_convert_fusion.1
  23.4 0.1 broadcast_add_fusion
  23.5 91.3 %all-gather.4.cloned.1.call-done = bf16[512,4096]{1,0:T(8,128)(2,1)} async-done(((bf16[512,256]{1,0:T(8,128)(2,1)}), bf16[512,4096]{1,0:T(8,128)(2,1)}) %all-gather.4.cloned.1.call-update) | async-done | bytes 4194320 | tf_op jit(solution)/shard_map/all_gather | solution.py:73
  114.8 3.0 convolution_convert_fusion
  117.8 1.1 copy.112
  119.0 4.5 all-to-all-start
  123.5 0.1 reshape.144
  123.6 0.1 copy.79
  123.7 0.1 mul.71
  123.9 4.3 scatter_custom_fusion.1
  128.3 11.1 %all-to-all-done = bf16[8,128,512]{2,1,0:T(8,128)(2,1)} async-done(((bf16[8,128,512]{2,1,0:T(8,128)(2,1)}), bf16[8,128,512]{2,1,0:T(8,128)(2,1)}, u32[]{:S(2)}, u32[]{:S(2)}) %all-to-all-start) | async-done | bytes 1048608 | tf_op jit(solution)/shard_map/all_to_all | solution.py:20
  139.4 1.4 convert_reduce_fusion
  140.8 1.0 fusion.31
  141.8 0.6 broadcast_in_dim.87
  142.4 3.5 all-to-all-start.1
  146.0 0.1 broadcast_in_dim.85
  146.1 4.3 scatter_custom_fusion
  150.5 0.1 broadcast_in_dim.82
  150.6 0.3 all-to-all-done.1
  150.9 0.1 fusion.33
  151.0 5.4 %gather_fusion = bf16[1536,512]{1,0:T(8,128)(2,1)} fusion(bf16[128,512]{1,0:T(8,128)(2,1)S(1)} %fusion.33, s32[2048]{0:T(1024)S(1)} %pad_clamp_fusion), kind=kCustom, calls=%fused_computation | custom fusion | bytes 3151872 | tf_op jit(solution)/shard_map/jit(_take)/gather | solution.py:100
  156.5 1.7 select_select_fusion
  158.2 81.1 %all_to_all.21 = bf16[16,2,48,512]{3,2,1,0:T(8,128)(2,1)S(1)} all-to-all(bf16[16,2,48,512]{3,2,1,0:T(8,128)(2,1)S(1)} %select_select_fusion), channel_id=1, replica_groups=mesh['rep'=2,'ep'=16,'tp'=8] {'ep'}, dimensions={0} | all-to-all | bytes 3145728 | tf_op jit(solution)/shard_map/all_to_all | solution.py:103
  239.3 1.3 copy.81
  240.6 0.2 all-gather.8.cloned.1.call-start
  240.9 68.9 %all-gather.6.cloned.1.call-done = bf16[16,2,48,4096]{3,2,0,1:T(8,128)(2,1)} async-done(((bf16[16,2,48,512]{3,2,0,1:T(8,128)(2,1)}), bf16[16,2,48,4096]{3,2,0,1:T(8,128)(2,1)}) %all-gather.6.cloned.1.call-update) | async-done | bytes 12582928 | tf_op jit(solution)/shard_map/all_gather | solution.py:102
  309.8 7.5 %fusion.6 = f32[2,16,48,192]{3,2,1,0:T(8,128)S(1)} fusion(bf16[16,2,48,4096]{3,2,0,1:T(8,128)(2,1)} %all-gather.6.cloned.1.call-done, bf16[2,4096,192]{1,2,0:T(8,128)(2,1)} %param.21), kind=kOutput, calls=%fused_computation.11 | convolution fusion | flops 2415919104 | bytes 16908288 | tf_op jit(solution)/shard_map/secd,edf->secf/dot_general | solution.py:114
  317.3 9.1 %fusion.14 = bf16[16,2,48,192]{3,2,0,1:T(8,128)(2,1)} fusion(f32[2,16,48,192]{3,2,1,0:T(8,128)S(1)} %fusion.6, bf16[16,2,48,4096]{3,2,0,1:T(8,128)(2,1)} %all-gather.6.cloned.1.call-done, bf16[2,4096,192]{1,2,0:T(8,128)(2,1)S(1)} %copy-done.4), kind=kOutput, calls=%fused_computation.19 | convolution fusion | flops 2417688576 | bytes 17498112 | tf_op jit(solution)/shard_map/secd,edf->secf/dot_general | solution.py:117
  326.3 3.2 copy.82
  329.6 73.9 %all-gather.8.cloned.1.call-done = bf16[16,2,48,1536]{2,0,1,3:T(8,128)(2,1)} async-done(((bf16[16,2,48,192]{2,0,1,3:T(8,128)(2,1)}), bf16[16,2,48,1536]{2,0,1,3:T(8,128)(2,1)}) %all-gather.8.cloned.1.call-update) | async-done | bytes 4718608 | tf_op jit(solution)/shard_map/all_gather | solution.py:119
  403.5 10.3 %fusion.18 = bf16[16,2,48,512]{3,2,0,1:T(8,128)(2,1)} fusion(bf16[2,1536,512]{2,1,0:T(8,128)(2,1)S(1)} %copy-done, bf16[16,2,48,1536]{2,0,1,3:T(8,128)(2,1)} %all-gather.8.cloned.1.call-done), kind=kOutput, calls=%fused_computation.26 | convolution fusion | flops 2416705536 | bytes 9437184 | tf_op jit(solution)/shard_map/secf,efd->secd/dot_general | solution.py:120
  413.9 2.7 copy.84
  416.6 12.5 %all-to-all-start.3 = ((bf16[16,2,48,512]{3,2,1,0:T(8,128)(2,1)}), bf16[16,2,48,512]{3,2,1,0:T(8,128)(2,1)}, u32[]{:S(2)}, u32[]{:S(2)}) async-start(bf16[16,2,48,512]{3,2,1,0:T(8,128)(2,1)} %copy.84), calls=%async_computation.3 | async-start | bytes 3145728 | tf_op jit(solution)/shard_map/all_to_all | solution.py:123
  429.2 0.1 copy.78
  429.4 0.1 copy.89
  429.5 74.0 %all-to-all-done.3 = bf16[16,2,48,512]{3,2,1,0:T(8,128)(2,1)} async-done(((bf16[16,2,48,512]{3,2,1,0:T(8,128)(2,1)}), bf16[16,2,48,512]{3,2,1,0:T(8,128)(2,1)}, u32[]{:S(2)}, u32[]{:S(2)}) %all-to-all-start.3) | async-done | bytes 1572896 | tf_op jit(solution)/shard_map/all_to_all | solution.py:123
  503.5 6.7 %gather_fusion.1 = bf16[1024,512]{1,0:T(8,128)(2,1)} fusion(bf16[1536,512]{1,0:T(8,128)(2,1)} %bitcast.101, s32[1024]{0:T(1024)S(1)} %broadcast_clamp_fusion), kind=kCustom, calls=%fused_computation.1 | custom fusion | bytes 2101248 | tf_op jit(solution)/shard_map/jit(_take)/gather | solution.py:127
  510.2 1.7 fusion.8
  512.0 0.7 fusion.34
  (35 shorter events, 0.6 us)
Async XLA Ops:
  6.5 397.0 %copy-start = (bf16[2,1536,512]{2,1,0:T(8,128)(2,1)S(1)}, bf16[2,1536,512]{2,1,0:T(8,128)(2,1)}, u32[]{:S(2)}) copy-start(bf16[2,1536,512]{2,1,0:T(8,128)(2,1)} %param.23) | copy-start | bytes 9437188
  6.6 14.9 %copy-start.5 = (bf16[128,256]{1,0:T(8,128)(2,1)S(1)}, bf16[128,256]{1,0:T(8,128)(2,1)}, u32[]{:S(2)}) copy-start(bf16[128,256]{1,0:T(8,128)(2,1)} %param.15) | copy-start | bytes 196612
  6.6 108.3 %all-gather.4.cloned.1.call-start = ((), (), s32[]{:S(2)}) async-start(), calls=%async_computation.4 | async-start | bytes 4456448 | tf_op jit(solution)/shard_map/all_gather | solution.py:73
  117.8 5.7 %copy-start.1 = (s32[128,8]{0,1:T(8,128)S(1)}, s32[128,8]{0,1:T(8,128)}, u32[]{:S(2)}) copy-start(s32[128,8]{0,1:T(8,128)} %param.19) | copy-start | bytes 12292
  119.0 32.0 %copy-start.3 = (f32[512]{0:T(512)S(1)}, f32[512]{0:T(512)}, u32[]{:S(2)}) copy-start(f32[512]{0:T(512)} %param.18) | copy-start | bytes 6148
  119.0 20.4 %all-to-all-start = ((bf16[8,128,512]{2,1,0:T(8,128)(2,1)}), bf16[8,128,512]{2,1,0:T(8,128)(2,1)}, u32[]{:S(2)}, u32[]{:S(2)}) async-start(bf16[8,128,512]{2,1,0:T(8,128)(2,1)} %bitcast.125), calls=%async_computation | async-start | bytes 2097152 | tf_op jit(solution)/shard_map/all_to_all | solution.py:20
  142.4 8.5 %all-to-all-start.1 = ((f32[8,1,128]{2,1,0:T(1,128)}), f32[8,1,128]{2,1,0:T(1,128)S(1)}, u32[]{:S(2)}, u32[]{:S(2)}) async-start(f32[8,1,128]{2,1,0:T(1,128)} %broadcast_in_dim.87), calls=%async_computation.1 | async-start | bytes 8192 | tf_op jit(solution)/shard_map/all_to_all | solution.py:26
  145.9 163.8 %all-gather.6.cloned.1.call-start = ((), (), s32[]{:S(2)}) async-start(), calls=%async_computation.5 | async-start | bytes 14155776 | tf_op jit(solution)/shard_map/all_gather | solution.py:102
  240.6 162.9 %all-gather.8.cloned.1.call-start = ((), (), s32[]{:S(2)}) async-start(), calls=%async_computation.6 | async-start | bytes 14155776 | tf_op jit(solution)/shard_map/all_gather | solution.py:119
  309.8 7.5 %copy-start.4 = (bf16[2,4096,192]{1,2,0:T(8,128)(2,1)S(1)}, bf16[2,4096,192]{1,2,0:T(8,128)(2,1)}, u32[]{:S(2)}) copy-start(bf16[2,4096,192]{1,2,0:T(8,128)(2,1)} %param.22) | copy-start | bytes 9437188
  416.6 12.8 %copy-start.2 = (f32[128,8]{0,1:T(8,128)S(1)}, f32[128,8]{0,1:T(8,128)}, u32[]{:S(2)}) copy-start(f32[128,8]{0,1:T(8,128)} %param.20) | copy-start | bytes 12292
  416.6 87.0 %all-to-all-start.3 = ((bf16[16,2,48,512]{3,2,1,0:T(8,128)(2,1)}), bf16[16,2,48,512]{3,2,1,0:T(8,128)(2,1)}, u32[]{:S(2)}, u32[]{:S(2)}) async-start(bf16[16,2,48,512]{3,2,1,0:T(8,128)(2,1)} %copy.84), calls=%async_computation.3 | async-start | bytes 3145728 | tf_op jit(solution)/shard_map/all_to_all | solution.py:123
Sparse Core Ops, SparseCore 0:
  9.1 105.6 all-gather.3
  240.8 68.9 all-gather.5
  329.7 73.7 all-gather.7
where the time goes:
time: 520 us; the launch traced here: 519 us
  waiting for transfers between devices  320 us (62%)
  blocking collectives  81.1 us (16%)
  matrix products  36.5 us (7%)
  local copies, waits for them, and re-layouts  31.8 us (6%)
  starting transfers between devices  20.9 us (4%)
  other arithmetic  14.3 us (3%)
  between operations  14.2 us (3%)
    all_gather x1, waiting for transfers between devices, shards(): lax.all_gather(out_weight, 'ep', axis=1, tiled=True)  91.3 us
    all_to_all x1, blocking collectives, shards(): lax.all_to_all(taken.reshape(ep_count, local_experts, capacity, normed.sh...  81.1 us
    all_to_all x1, waiting for transfers between devices, shards(): lax.all_to_all(produced.astype(jnp.bfloat16), 'ep', split_axis=0, concat_...  74 us
    all_gather x1, waiting for transfers between devices, shards(): hidden_all = lax.all_gather(active, 'tp', axis=3, tiled=True)  73.9 us
    all_gather x1, waiting for transfers between devices, shards(): lax.all_gather(lax.all_to_all(taken.reshape(ep_count, local_experts, capa...  68.9 us
    all_to_all x1, starting transfers between devices, shards(): lax.all_to_all(produced.astype(jnp.bfloat16), 'ep', split_axis=0, concat_...  12.5 us
    all_to_all x1, waiting for transfers between devices, sent_and_summed(): lax.all_to_all(blocks, axis, split_axis=0, concat_axis=0, tiled=True)  11.1 us
  transfers between devices with their start and end apart: 6, of which 6 were waited for; matrix products, arithmetic and copies ran while one was open for 5% of the time, Pallas kernels for 0%

commit v1 on v0

--- a/solution.py
+++ b/solution.py
@@ -116,7 +116,16 @@
     )
     up_val = jnp.einsum("secd,edf->secf", arrived, up_weight, preferred_element_type=jnp.float32)
     active = (jax.nn.silu(gate_val) * up_val).astype(jnp.bfloat16)
-    hidden_all = lax.all_gather(active, "tp", axis=3, tiled=True)
+    ways = lax.axis_size("tp")
+    up = [(d, (d + 1) % ways) for d in range(ways)]
+    down = [(d, (d - 1) % ways) for d in range(ways)]
+    earlier_2, later = ([active], [active])
+    for _ in range(ways // 2):
+        earlier_2.append(lax.ppermute(earlier_2[-1], "tp", up))
+    for _ in range((ways - 1) // 2):
+        later.append(lax.ppermute(later[-1], "tp", down))
+    line = jnp.concatenate([*earlier_2[::-1], *later[1:]], axis=3)
+    hidden_all = jnp.roll(line, (lax.axis_index("tp") - ways // 2) * active.shape[3], axis=3)
     produced = jnp.einsum(
         "secf,efd->secd", hidden_all, down_weight, preferred_element_type=jnp.float32
     )

time: 520 us -> 500 us (0.962)
  waiting for transfers between devices: 320 us -> 280 us
  local copies, waits for them, and re-layouts: 31.8 us -> 47.4 us
  starting transfers between devices: 20.9 us -> 27.3 us
  matrix products: 36.5 us -> 30.5 us
    all_gather x1 -> x0, waiting for transfers between devices: 73.9 us -> none  [shards(): hidden_all = lax.all_gather(active, 'tp', axis=3, tiled=True)]
    ppermute x0 -> x7, waiting for transfers between devices: none -> 41.9 us  [the longest x4 41.6 us: shards(): earlier_2.append(lax.ppermute(earlier_2[-1], 'tp', up))]
    concatenate x0 -> x1, local copies, waits for them, and re-layouts: none -> 17.8 us  [shards(): jnp.roll(line, (lax.axis_index('tp') - ways // 2) * active.shape[3], axis=3)]
    all_to_all x1, waiting for transfers between devices: 74 us -> 64.9 us  [shards(): lax.all_to_all(produced.astype(jnp.bfloat16), 'ep', split_axis=0, concat_...]
    ppermute x0 -> x7, starting transfers between devices: none -> 6.72 us  [the longest x3 6.41 us: shards(): later.append(lax.ppermute(later[-1], 'tp', down))]
    dot_general x1, matrix products: 10.3 us -> 5.14 us  [shards(): jnp.einsum('secf,efd->secd', hidden_all, down_weight, preferred_element_t...]
  transfers between devices with their start and end apart: 6 -> 12, of which waited for: 6 -> 10; matrix products, arithmetic and copies ran while one was open for 5% -> 5% of each run, Pallas kernels for 0% -> 0%
where the time goes in v1:
time: 500 us; the launch traced here: 495 us
  waiting for transfers between devices  280 us (56%)
  blocking collectives  81.1 us (16%)
  local copies, waits for them, and re-layouts  47.4 us (9%)
  matrix products  30.5 us (6%)
  starting transfers between devices  27.3 us (5%)
  between operations  14.6 us (3%)
  other arithmetic  14.3 us (3%)
    all_gather x1, waiting for transfers between devices, shards(): lax.all_gather(out_weight, 'ep', axis=1, tiled=True)  91.3 us
    all_to_all x1, blocking collectives, shards(): lax.all_to_all(taken.reshape(ep_count, local_experts, capacity, normed.sh...  81.1 us
    all_gather x1, waiting for transfers between devices, shards(): lax.all_gather(lax.all_to_all(taken.reshape(ep_count, local_experts, capa...  69.1 us
    all_to_all x1, waiting for transfers between devices, shards(): lax.all_to_all(produced.astype(jnp.bfloat16), 'ep', split_axis=0, concat_...  64.9 us
    ppermute x4, waiting for transfers between devices, shards(): earlier_2.append(lax.ppermute(earlier_2[-1], 'tp', up))  41.6 us
    concatenate x1, local copies, waits for them, and re-layouts, shards(): jnp.roll(line, (lax.axis_index('tp') - ways // 2) * active.shape[3], axis=3)  17.8 us
    all_to_all x1, starting transfers between devices, shards(): lax.all_to_all(produced.astype(jnp.bfloat16), 'ep', split_axis=0, concat_...  12.5 us
    all_to_all x1, waiting for transfers between devices, sent_and_summed(): lax.all_to_all(blocks, axis, split_axis=0, concat_axis=0, tiled=True)  11.1 us
  transfers between devices with their start and end apart: 12, of which 10 were waited for; matrix products, arithmetic and copies ran while one was open for 5% of the time, Pallas kernels for 0%

profile of v1, /device:TPU:40, one launch (start us, length us, event | category | flops | bytes accessed | tf_op | source)
XLA Modules:
  0.0 494.6 jit_solution(16642018960827150715)
XLA Ops:
  6.6 0.7 all-gather.3.cloned.1.call-update
  8.1 0.8 copy.67
  9.0 9.0 %reduce-window.6 = s32[32,8,128]{2,1,0:T(8,128)S(1)} reduce-window(s32[32,8,128]{2,1,0:T(8,128)S(1)} %fusion.40, s32[]{:T(128)} %constant.93.clone.1), window={size=1x1x128 pad=0_0x0_0x127_0}, to_apply=%region_3.4 | reduce-window | flops 4161536 | bytes 262148 | tf_op jit(solution)/shard_map/reduce-window
  18.1 0.1 copy.69
  18.5 1.2 fusion.66
  19.7 1.8 fusion.27
  21.5 1.9 convolution_convert_fusion.1
  23.5 91.3 %all-gather.3.cloned.1.call-done = bf16[512,4096]{1,0:T(8,128)(2,1)} async-done(((bf16[512,256]{1,0:T(8,128)(2,1)}), bf16[512,4096]{1,0:T(8,128)(2,1)}) %all-gather.3.cloned.1.call-update) | async-done | bytes 4194320 | tf_op jit(solution)/shard_map/all_gather | solution.py:73
  114.8 3.0 convolution_convert_fusion
  117.8 1.1 copy.98
  119.0 4.5 all-to-all-start
  123.9 4.3 scatter_custom_fusion.1
  128.2 11.1 %all-to-all-done = bf16[8,128,512]{2,1,0:T(8,128)(2,1)} async-done(((bf16[8,128,512]{2,1,0:T(8,128)(2,1)}), bf16[8,128,512]{2,1,0:T(8,128)(2,1)}, u32[]{:S(2)}, u32[]{:S(2)}) %all-to-all-start) | async-done | bytes 1048608 | tf_op jit(solution)/shard_map/all_to_all | solution.py:20
  139.4 1.4 convert_reduce_fusion
  140.8 1.0 fusion.31
  141.8 0.6 broadcast_in_dim.87
  142.4 3.5 all-to-all-start.1
  146.1 4.3 scatter_custom_fusion
  150.6 0.3 all-to-all-done.1
  151.0 5.4 %gather_fusion = bf16[1536,512]{1,0:T(8,128)(2,1)} fusion(bf16[128,512]{1,0:T(8,128)(2,1)S(1)} %fusion.33, s32[2048]{0:T(1024)S(1)} %pad_clamp_fusion), kind=kCustom, calls=%fused_computation | custom fusion | bytes 3151872 | tf_op jit(solution)/shard_map/jit(_take)/gather | solution.py:100
  156.5 1.7 select_select_fusion
  158.2 81.1 %all_to_all.21 = bf16[16,2,48,512]{3,2,1,0:T(8,128)(2,1)S(1)} all-to-all(bf16[16,2,48,512]{3,2,1,0:T(8,128)(2,1)S(1)} %select_select_fusion), channel_id=1, replica_groups=mesh['rep'=2,'ep'=16,'tp'=8] {'ep'}, dimensions={0} | all-to-all | bytes 3145728 | tf_op jit(solution)/shard_map/all_to_all | solution.py:103
  239.3 1.3 copy.75
  240.6 69.1 %all-gather.5.cloned.1.call-done = bf16[16,2,48,4096]{3,2,0,1:T(8,128)(2,1)} async-done(((bf16[16,2,48,512]{3,2,0,1:T(8,128)(2,1)}), bf16[16,2,48,4096]{3,2,0,1:T(8,128)(2,1)}) %all-gather.5.cloned.1.call-update) | async-done | bytes 12582928 | tf_op jit(solution)/shard_map/all_gather | solution.py:102
  309.8 7.5 %fusion.6 = f32[2,16,48,192]{3,2,1,0:T(8,128)S(1)} fusion(bf16[16,2,48,4096]{3,2,0,1:T(8,128)(2,1)} %all-gather.5.cloned.1.call-done, bf16[2,4096,192]{1,2,0:T(8,128)(2,1)} %param.21), kind=kOutput, calls=%fused_computation.11 | convolution fusion | flops 2415919104 | bytes 16908288 | tf_op jit(solution)/shard_map/secd,edf->secf/dot_general | solution.py:114
  317.3 8.2 %fusion.14 = bf16[16,2,48,192]{3,2,0,1:T(8,128)(2,1)S(1)} fusion(f32[2,16,48,192]{3,2,1,0:T(8,128)S(1)} %fusion.6, bf16[16,2,48,4096]{3,2,0,1:T(8,128)(2,1)} %all-gather.5.cloned.1.call-done, bf16[2,4096,192]{1,2,0:T(8,128)(2,1)S(1)} %copy-done.8), kind=kOutput, calls=%fused_computation.19 | convolution fusion | flops 2417688576 | bytes 17498112 | tf_op jit(solution)/shard_map/secd,edf->secf/dot_general | solution.py:117
  325.5 0.3 collective-permute-start
  325.8 0.6 copy-done.1
  326.4 2.1 collective-permute-start.4
  328.5 9.7 %collective-permute-done = bf16[16,2,48,192]{3,2,0,1:T(8,128)(2,1)S(1)} collective-permute-done((bf16[16,2,48,192]{3,2,0,1:T(8,128)(2,1)S(1)}, bf16[16,2,48,192]{3,2,0,1:T(8,128)(2,1)S(1)}, u32[]{:S(2)}, u32[]{:S(2)}) %collective-permute-start) | collective-permute-done | bytes 589856 | tf_op jit(solution)/shard_map/ppermute | solution.py:124
  338.2 0.9 copy-done.2
  339.0 2.1 collective-permute-start.5
  341.2 9.6 %collective-permute-done.1 = bf16[16,2,48,192]{3,2,0,1:T(8,128)(2,1)S(1)} collective-permute-done((bf16[16,2,48,192]{3,2,0,1:T(8,128)(2,1)S(1)}, bf16[16,2,48,192]{3,2,0,1:T(8,128)(2,1)S(1)}, u32[]{:S(2)}, u32[]{:S(2)}) %collective-permute-start.1) | collective-permute-done | bytes 589856 | tf_op jit(solution)/shard_map/ppermute | solution.py:124
  350.8 0.9 copy-done.4
  351.7 2.2 collective-permute-start.6
  353.9 9.6 %collective-permute-done.2 = bf16[16,2,48,192]{3,2,0,1:T(8,128)(2,1)} collective-permute-done((bf16[16,2,48,192]{3,2,0,1:T(8,128)(2,1)S(1)}, bf16[16,2,48,192]{3,2,0,1:T(8,128)(2,1)}, u32[]{:S(2)}, u32[]{:S(2)}) %collective-permute-start.2) | collective-permute-done | bytes 589856 | tf_op jit(solution)/shard_map/ppermute | solution.py:124
  363.5 0.2 collective-permute-done.6
  363.7 12.7 %collective-permute-done.3 = bf16[16,2,48,192]{3,2,0,1:T(8,128)(2,1)} collective-permute-done((bf16[16,2,48,192]{3,2,0,1:T(8,128)(2,1)}, bf16[16,2,48,192]{3,2,0,1:T(8,128)(2,1)}, u32[]{:S(2)}, u32[]{:S(2)}) %collective-permute-start.3) | collective-permute-done | bytes 589856 | tf_op jit(solution)/shard_map/ppermute | solution.py:124
  376.5 17.8 %concatenate.6 = bf16[16,2,48,3072]{3,2,0,1:T(8,128)(2,1)} concatenate(bf16[16,2,48,192]{3,2,0,1:T(8,128)(2,1)} %collective-permute-done.3, bf16[16,2,48,192]{3,2,0,1:T(8,128)(2,1)} %collective-permute-done.2, bf16[16,2,48,192]{3,2,0,1:T(8,128)(2,1)} %copy-done.4, bf16[16,2,48,192]{3,2,0,1:T(8,128)(2,1)} %copy-done.2, bf16[16,2,48,192]{3,2,0,1:T(8,128)(2,1)} %copy-done.1, ...), dimensions={3} | concatenate | bytes 18874368 | tf_op jit(solution)/shard_map/jit(_roll_dynamic)/concatenate | solution.py:128
  394.3 5.1 %fusion.18 = bf16[16,2,48,512]{3,2,0,1:T(8,128)(2,1)S(1)} fusion(bf16[2,1536,512]{2,1,0:T(8,128)(2,1)S(1)} %copy-done, bf16[16,2,48,3072]{3,2,0,1:T(8,128)(2,1)} %concatenate.6, s32[]{:T(128)S(6)} %select_n.78), kind=kOutput, calls=%fused_computation.26 | convolution fusion | flops 2416705536 | bytes 9437188 | tf_op jit(solution)/shard_map/secf,efd->secd/dot_general | solution.py:129
  399.4 1.3 copy.76
  400.7 12.5 %all-to-all-start.3 = ((bf16[16,2,48,512]{3,2,1,0:T(8,128)(2,1)}), bf16[16,2,48,512]{3,2,1,0:T(8,128)(2,1)}, u32[]{:S(2)}, u32[]{:S(2)}) async-start(bf16[16,2,48,512]{3,2,1,0:T(8,128)(2,1)} %copy.76), calls=%async_computation.3 | async-start | bytes 3145728 | tf_op jit(solution)/shard_map/all_to_all | solution.py:132
  413.4 0.1 copy.72
  413.5 0.1 copy.81
  413.7 64.9 %all-to-all-done.3 = bf16[16,2,48,512]{3,2,1,0:T(8,128)(2,1)} async-done(((bf16[16,2,48,512]{3,2,1,0:T(8,128)(2,1)}), bf16[16,2,48,512]{3,2,1,0:T(8,128)(2,1)}, u32[]{:S(2)}, u32[]{:S(2)}) %all-to-all-start.3) | async-done | bytes 1572896 | tf_op jit(solution)/shard_map/all_to_all | solution.py:132
  478.6 6.7 %gather_fusion.1 = bf16[1024,512]{1,0:T(8,128)(2,1)} fusion(bf16[1536,512]{1,0:T(8,128)(2,1)} %bitcast.101, s32[1024]{0:T(1024)S(1)} %broadcast_clamp_fusion), kind=kCustom, calls=%fused_computation.1 | custom fusion | bytes 2101248 | tf_op jit(solution)/shard_map/jit(_take)/gather | solution.py:136
  485.3 1.7 fusion.8
  487.1 0.7 fusion.34
  (54 shorter events, 1.5 us)
Async XLA Ops:
  6.5 387.7 %copy-start = (bf16[2,1536,512]{2,1,0:T(8,128)(2,1)S(1)}, bf16[2,1536,512]{2,1,0:T(8,128)(2,1)}, u32[]{:S(2)}) copy-start(bf16[2,1536,512]{2,1,0:T(8,128)(2,1)} %param.23) | copy-start | bytes 9437188
  6.6 14.9 %copy-start.9 = (bf16[128,256]{1,0:T(8,128)(2,1)S(1)}, bf16[128,256]{1,0:T(8,128)(2,1)}, u32[]{:S(2)}) copy-start(bf16[128,256]{1,0:T(8,128)(2,1)} %param.15) | copy-start | bytes 196612
  6.6 108.3 %all-gather.3.cloned.1.call-start = ((), (), s32[]{:S(2)}) async-start(), calls=%async_computation.4 | async-start | bytes 4456448 | tf_op jit(solution)/shard_map/all_gather | solution.py:73
  117.8 5.7 %copy-start.5 = (s32[128,8]{0,1:T(8,128)S(1)}, s32[128,8]{0,1:T(8,128)}, u32[]{:S(2)}) copy-start(s32[128,8]{0,1:T(8,128)} %param.19) | copy-start | bytes 12292
  119.0 32.0 %copy-start.7 = (f32[512]{0:T(512)S(1)}, f32[512]{0:T(512)}, u32[]{:S(2)}) copy-start(f32[512]{0:T(512)} %param.18) | copy-start | bytes 6148
  119.0 20.4 %all-to-all-start = ((bf16[8,128,512]{2,1,0:T(8,128)(2,1)}), bf16[8,128,512]{2,1,0:T(8,128)(2,1)}, u32[]{:S(2)}, u32[]{:S(2)}) async-start(bf16[8,128,512]{2,1,0:T(8,128)(2,1)} %bitcast.125), calls=%async_computation | async-start | bytes 2097152 | tf_op jit(solution)/shard_map/all_to_all | solution.py:20
  142.4 8.5 %all-to-all-start.1 = ((f32[8,1,128]{2,1,0:T(1,128)}), f32[8,1,128]{2,1,0:T(1,128)S(1)}, u32[]{:S(2)}, u32[]{:S(2)}) async-start(f32[8,1,128]{2,1,0:T(1,128)} %broadcast_in_dim.87), calls=%async_computation.1 | async-start | bytes 8192 | tf_op jit(solution)/shard_map/all_to_all | solution.py:26
  145.9 163.8 %all-gather.5.cloned.1.call-start = ((), (), s32[]{:S(2)}) async-start(), calls=%async_computation.5 | async-start | bytes 14155776 | tf_op jit(solution)/shard_map/all_gather | solution.py:102
  309.8 7.5 %copy-start.8 = (bf16[2,4096,192]{1,2,0:T(8,128)(2,1)S(1)}, bf16[2,4096,192]{1,2,0:T(8,128)(2,1)}, u32[]{:S(2)}) copy-start(bf16[2,4096,192]{1,2,0:T(8,128)(2,1)} %param.22) | copy-start | bytes 9437188
  325.5 0.9 copy-start.1
  325.5 12.7 %collective-permute-start = (bf16[16,2,48,192]{3,2,0,1:T(8,128)(2,1)S(1)}, bf16[16,2,48,192]{3,2,0,1:T(8,128)(2,1)S(1)}, u32[]{:S(2)}, u32[]{:S(2)}) collective-permute-start(bf16[16,2,48,192]{3,2,0,1:T(8,128)(2,1)S(1)} %fusion.14), channel_id=1, source_target_pairs={{0,1},{1,2},{2,3},{3,4},{4,5},{5,6},{6,7},{7,0},{8,9},{9,10},{10,1... | collective-permute-start | bytes 1769480 | tf_op jit(solution)/shard_map/ppermute | solution.py:124
  326.4 11.8 %collective-permute-start.4 = (bf16[16,2,48,192]{3,2,0,1:T(8,128)(2,1)S(1)}, bf16[16,2,48,192]{3,2,0,1:T(8,128)(2,1)S(1)}, u32[]{:S(2)}, u32[]{:S(2)}) collective-permute-start(bf16[16,2,48,192]{3,2,0,1:T(8,128)(2,1)S(1)} %fusion.14), channel_id=1, source_target_pairs={{0,7},{1,0},{2,1},{3,2},{4,3},{5,4},{6,5},{7,6},{8,15},{9,8},{10,9... | collective-permute-start | bytes 1769480 | tf_op jit(solution)/shard_map/ppermute | solution.py:126
  338.2 0.9 copy-start.2
  338.2 12.6 %collective-permute-start.1 = (bf16[16,2,48,192]{3,2,0,1:T(8,128)(2,1)S(1)}, bf16[16,2,48,192]{3,2,0,1:T(8,128)(2,1)S(1)}, u32[]{:S(2)}, u32[]{:S(2)}) collective-permute-start(bf16[16,2,48,192]{3,2,0,1:T(8,128)(2,1)S(1)} %collective-permute-done), channel_id=1, source_target_pairs={{0,1},{1,2},{2,3},{3,4},{4,5},{5,6},{6,7},{7,0},{8,9},{9,10},{10,1... | collective-permute-start | bytes 1769480 | tf_op jit(solution)/shard_map/ppermute | solution.py:124
  339.0 11.7 %copy-start.3 = (bf16[16,2,48,192]{3,2,0,1:T(8,128)(2,1)}, bf16[16,2,48,192]{3,2,0,1:T(8,128)(2,1)S(1)}, u32[]{:S(2)}) copy-start(bf16[16,2,48,192]{3,2,0,1:T(8,128)(2,1)S(1)} %collective-permute-done.4) | copy-start | bytes 1769476
  339.0 11.8 %collective-permute-start.5 = (bf16[16,2,48,192]{3,2,0,1:T(8,128)(2,1)S(1)}, bf16[16,2,48,192]{3,2,0,1:T(8,128)(2,1)}, u32[]{:S(2)}, u32[]{:S(2)}) collective-permute-start(bf16[16,2,48,192]{3,2,0,1:T(8,128)(2,1)S(1)} %collective-permute-done.4), channel_id=1, source_target_pairs={{0,7},{1,0},{2,1},{3,2},{4,3},{5,4},{6,5},{7,6},{8,15},{9,8},{10,9... | collective-permute-start | bytes 1769480 | tf_op jit(solution)/shard_map/ppermute | solution.py:126
  350.8 0.9 copy-start.4
  350.8 12.7 %collective-permute-start.2 = (bf16[16,2,48,192]{3,2,0,1:T(8,128)(2,1)S(1)}, bf16[16,2,48,192]{3,2,0,1:T(8,128)(2,1)}, u32[]{:S(2)}, u32[]{:S(2)}) collective-permute-start(bf16[16,2,48,192]{3,2,0,1:T(8,128)(2,1)S(1)} %collective-permute-done.1), channel_id=1, source_target_pairs={{0,1},{1,2},{2,3},{3,4},{4,5},{5,6},{6,7},{7,0},{8,9},{9,10},{10,1... | collective-permute-start | bytes 1769480 | tf_op jit(solution)/shard_map/ppermute | solution.py:124
  351.7 12.0 %collective-permute-start.6 = (bf16[16,2,48,192]{3,2,0,1:T(8,128)(2,1)}, bf16[16,2,48,192]{3,2,0,1:T(8,128)(2,1)}, u32[]{:S(2)}, u32[]{:S(2)}) collective-permute-start(bf16[16,2,48,192]{3,2,0,1:T(8,128)(2,1)} %collective-permute-done.5), channel_id=1, source_target_pairs={{0,7},{1,0},{2,1},{3,2},{4,3},{5,4},{6,5},{7,6},{8,15},{9,8},{10,9... | collective-permute-start | bytes 1769480 | tf_op jit(solution)/shard_map/ppermute | solution.py:126
  363.5 12.9 %collective-permute-start.3 = (bf16[16,2,48,192]{3,2,0,1:T(8,128)(2,1)}, bf16[16,2,48,192]{3,2,0,1:T(8,128)(2,1)}, u32[]{:S(2)}, u32[]{:S(2)}) collective-permute-start(bf16[16,2,48,192]{3,2,0,1:T(8,128)(2,1)} %collective-permute-done.2), channel_id=1, source_target_pairs={{0,1},{1,2},{2,3},{3,4},{4,5},{5,6},{6,7},{7,0},{8,9},{9,10},{10,1... | collective-permute-start | bytes 1769480 | tf_op jit(solution)/shard_map/ppermute | solution.py:124
  400.7 12.8 %copy-start.6 = (f32[128,8]{0,1:T(8,128)S(1)}, f32[128,8]{0,1:T(8,128)}, u32[]{:S(2)}) copy-start(f32[128,8]{0,1:T(8,128)} %param.20) | copy-start | bytes 12292
  400.7 77.9 %all-to-all-start.3 = ((bf16[16,2,48,512]{3,2,1,0:T(8,128)(2,1)}), bf16[16,2,48,512]{3,2,1,0:T(8,128)(2,1)}, u32[]{:S(2)}, u32[]{:S(2)}) async-start(bf16[16,2,48,512]{3,2,1,0:T(8,128)(2,1)} %copy.76), calls=%async_computation.3 | async-start | bytes 3145728 | tf_op jit(solution)/shard_map/all_to_all | solution.py:132
Sparse Core Ops, SparseCore 0:
  9.1 105.6 all-gather.2
  240.8 68.9 all-gather.4
